TPU v7x, 32 devices: a whole 2x2x4 slice. The times are simulated.
32 devices in a mesh: mp: 8 (over y, x, core), hidden: 4 (over z).
Axes of the slice: x: 2, y: 2, z: 4, core: 2. Of those that a mesh axis runs over, the one named last changes fastest.
Arguments:
- states: bfloat16 [512, 16384], P(None, 'mp'), may hold values from -6 to 6
- gate_codes: bfloat16 [16384, 26624], P('mp', 'hidden'), may hold values from -127 to 127, as said below
- gate_scales: float32 [128, 26624], P('mp', 'hidden'), may hold values from 7.8125e-05 to 0.000703125
- up_codes: bfloat16 [16384, 26624], P('mp', 'hidden'), may hold values from -127 to 127, as said below
- up_scales: float32 [128, 26624], P('mp', 'hidden'), may hold values from 7.8125e-05 to 0.000703125
- down_codes: bfloat16 [26624, 16384], P('hidden', 'mp'), may hold values from -127 to 127, as said below
- down_scales: float32 [208, 16384], P('hidden', 'mp'), may hold values from 1.2257258e-05 to 0.000110315326
Outputs:
- output: bfloat16 [512, 16384], P(None, 'mp')
Inputs may be any that keep to these rules, and one draw needn't show every extreme that they name: `gate_codes`: whole numbers. `up_codes`: whole numbers. `down_codes`: whole numbers.
All inputs are finite; a program needn't handle non-finite values. Where the computation divides by a largest or mean magnitude, that divisor is 1e-20 or more.
Results may differ from a plain program's by a relative error of at most 0.02.
Values may be sent and summed in bfloat16 or wider, within the bound.
A program may use at most 256 MiB of HBM per device.

v0:
```python
import jax
import jax.numpy as jnp
from jax import lax
from jax.sharding import PartitionSpec as P

BLOCK = 128
epsilon = 1e-06


def dequantize(quantized, scales):
    depth, columns = quantized.shape
    groups = scales.shape[0]
    blocks = quantized.astype(jnp.float32).reshape(groups, depth // groups, columns)
    return (blocks * scales[:, None, :]).reshape(depth, columns).astype(jnp.bfloat16)


def encode(values):
    row_count, columns = values.shape
    blocks = values.reshape(row_count, columns // BLOCK, BLOCK)
    maxima = (jnp.max(jnp.abs(blocks), axis=-1) + epsilon).astype(jnp.bfloat16)
    factor = 127.0 / maxima.astype(jnp.float32)
    codes = (blocks * factor[..., None]).astype(jnp.bfloat16)
    return (codes.reshape(row_count, columns), maxima)


def decode(codes, maxima):
    row_count, columns = codes.shape
    blocks = codes.astype(jnp.float32).reshape(row_count, columns // BLOCK, BLOCK)
    step_size = maxima.astype(jnp.float32) / 127.0
    return (blocks * step_size[..., None]).reshape(row_count, columns)


def body(states, gate_codes, gate_scales, up_codes, up_scales, down_codes, down_scales):
    gate_w = dequantize(gate_codes, gate_scales)
    up_w = dequantize(up_codes, up_scales)
    columns = gate_w.shape[1]
    row_count = states.shape[0]
    senders = lax.axis_size("mp")
    own_rows = row_count // senders
    gate_part = jnp.dot(states, gate_w, preferred_element_type=jnp.float32)
    up_part = jnp.dot(states, up_w, preferred_element_type=jnp.float32)
    gate_enc, gate_max = encode(gate_part)
    up_enc, up_max = encode(up_part)
    codes = jnp.concatenate([gate_enc, up_enc], axis=1)
    scales = jnp.concatenate([gate_max, up_max], axis=1)
    got_codes, got_scales = (
        lax.all_to_all(codes, "mp", split_axis=0, concat_axis=0, tiled=True),
        lax.all_to_all(scales, "mp", split_axis=0, concat_axis=0, tiled=True),
    )
    summed = decode(got_codes, got_scales).reshape(senders, own_rows, 2 * columns).sum(axis=0)
    swiglu = jax.nn.silu(summed[:, :columns]) * summed[:, columns:]
    act_codes, act_scales = encode(swiglu)
    all_codes, all_scales = (
        lax.all_gather(act_codes, "mp", axis=0, tiled=True),
        lax.all_gather(act_scales, "mp", axis=0, tiled=True),
    )
    activation = decode(all_codes, all_scales).astype(jnp.bfloat16)
    down_w = dequantize(down_codes, down_scales)
    whole_sum = lax.psum(
        jnp.dot(activation, down_w, preferred_element_type=jnp.float32).astype(jnp.bfloat16),
        "hidden",
    ).astype(jnp.float32)
    return (whole_sum + states.astype(jnp.float32)).astype(jnp.bfloat16)


def solution(mesh):
    in_specs = (
        P(None, "mp"),
        P("mp", "hidden"),
        P("mp", "hidden"),
        P("mp", "hidden"),
        P("mp", "hidden"),
        P("hidden", "mp"),
        P("hidden", "mp"),
    )
    out_specs = P(None, "mp")
    return jax.shard_map(body, mesh=mesh, in_specs=in_specs, out_specs=out_specs, check_vma=False)
```

profile of v0, /device:TPU:0, one launch (start us, length us, event | category | flops | bytes accessed | tf_op | source)
XLA Modules:
  0.0 518.5 jit_solution(13430339111039711883)
XLA Ops:
  6.5 0.0 copy-start
  6.5 19.5 %fusion.2 = bf16[2048,6656]{1,0:T(8,128)(2,1)} fusion(bf16[2048,6656]{1,0:T(8,128)(2,1)} %param.8, f32[16,6656]{1,0:T(8,128)} %param.9), kind=kLoop, calls=%fused_computation.5 | loop fusion | flops 40894464 | bytes 54951936 | tf_op jit(solution)/shard_map/convert_element_type | solution.py:14
  26.0 0.0 copy-done
  26.0 25.2 %bitcast_abs_fusion.1 = (f32[512,6656]{0,1:T(8,128)}, f32[6656,512]{1,0:T(8,128)}) fusion(bf16[2048,6656]{1,0:T(8,128)(2,1)} %fusion.2, bf16[512,2048]{1,0:T(8,128)(2,1)S(1)} %copy-done), kind=kOutput, calls=%fused_computation.13 | convolution fusion | flops 13962051584 | bytes 56623104 | tf_op jit(solution)/shard_map/dot_general | solution.py:40
  51.3 0.0 copy-start.2
  51.3 7.1 %reduce_max.27 = f32[512,52]{0,1:T(8,128)S(1)} reduce(f32[512,52,128]{0,2,1:T(8,128)} %bitcast.51, f32[]{:T(128)} %constant.7.clone.1), dimensions={2}, to_apply=%region_0.0 | reduce | flops 3381248 | bytes 13737988 | tf_op jit(solution)/shard_map/reduce_max | solution.py:20
  58.4 0.1 copy.41
  58.5 0.0 copy-done.2
  58.5 19.0 %fusion.1 = bf16[2048,6656]{1,0:T(8,128)(2,1)} fusion(bf16[2048,6656]{1,0:T(8,128)(2,1)} %param.10, f32[16,6656]{1,0:T(8,128)S(1)} %copy-done.2), kind=kLoop, calls=%fused_computation.3 | loop fusion | flops 40894464 | bytes 54951936 | tf_op jit(solution)/shard_map/convert_element_type | solution.py:14
  77.6 25.5 %bitcast_abs_fusion = (f32[512,6656]{0,1:T(8,128)}, f32[6656,512]{1,0:T(8,128)}) fusion(bf16[2048,6656]{1,0:T(8,128)(2,1)} %fusion.1, bf16[512,2048]{1,0:T(8,128)(2,1)S(1)} %copy-done), kind=kOutput, calls=%fused_computation.10 | convolution fusion | flops 13962051584 | bytes 56623104 | tf_op jit(solution)/shard_map/dot_general | solution.py:41
  103.1 7.0 %reduce_max.28 = f32[512,52]{0,1:T(8,128)S(1)} reduce(f32[512,52,128]{0,2,1:T(8,128)} %bitcast.52, f32[]{:T(128)} %constant.7.clone.1), dimensions={2}, to_apply=%region_1.0 | reduce | flops 3381248 | bytes 13737988 | tf_op jit(solution)/shard_map/reduce_max | solution.py:20
  110.1 0.1 copy.42
  110.3 0.8 pad_maximum_fusion.1
  111.0 5.2 %all-to-all-start.1 = ((bf16[8,64,104]{2,1,0:T(8,128)(2,1)}), bf16[8,64,104]{2,1,0:T(8,128)(2,1)S(1)}, u32[]{:S(2)}, u32[]{:S(2)}) async-start(bf16[8,64,104]{2,1,0:T(8,128)(2,1)} %pad_maximum_fusion.1), calls=%async_computation.1 | async-start | bytes 262144 | tf_op jit(solution)/shard_map/all_to_all | solution.py:48
  116.2 9.7 %fusion.4 = bf16[512,6656]{0,1:T(8,128)(2,1)} fusion(f32[6656,512]{1,0:T(8,128)} %get-tuple-element.14, f32[512,52]{0,1:T(8,128)S(1)} %get-tuple-element.5), kind=kLoop, calls=%fused_computation.12 | loop fusion | flops 6815744 | bytes 20553728 | tf_op jit(solution)/shard_map/convert_element_type | solution.py:22
  125.9 10.0 %copy.34 = bf16[512,6656]{1,0:T(8,128)(2,1)} copy(bf16[512,6656]{0,1:T(8,128)(2,1)} %fusion.4) | data formatting | bytes 13631488 | tf_op jit(solution)/shard_map/convert_element_type | solution.py:22
  135.9 9.6 %fusion.3 = bf16[512,6656]{0,1:T(8,128)(2,1)} fusion(f32[6656,512]{1,0:T(8,128)} %get-tuple-element.12, f32[512,52]{0,1:T(8,128)S(1)} %get-tuple-element.7), kind=kLoop, calls=%fused_computation.9 | loop fusion | flops 6815744 | bytes 20553728 | tf_op jit(solution)/shard_map/convert_element_type | solution.py:22
  145.5 9.8 %copy.35 = bf16[512,6656]{1,0:T(8,128)(2,1)} copy(bf16[512,6656]{0,1:T(8,128)(2,1)} %fusion.3) | data formatting | bytes 13631488 | tf_op jit(solution)/shard_map/convert_element_type | solution.py:22
  155.3 11.8 %pad_maximum_fusion = bf16[8,64,13312]{2,1,0:T(8,128)(2,1)} fusion(bf16[8,64,6656]{2,1,0:T(8,128)(2,1)} %bitcast.50, bf16[8,64,6656]{2,1,0:T(8,128)(2,1)} %bitcast.49), kind=kLoop, calls=%fused_computation.7 | loop fusion | flops 27262976 | bytes 27262976 | tf_op jit(solution)/shard_map/concatenate | solution.py:44
  167.1 0.0 all-to-all-done.1
  167.1 5.5 %all-to-all-start = ((bf16[8,64,13312]{2,1,0:T(8,128)(2,1)}), bf16[8,64,13312]{2,1,0:T(8,128)(2,1)}, u32[]{:S(2)}, u32[]{:S(2)}) async-start(bf16[8,64,13312]{2,1,0:T(8,128)(2,1)} %pad_maximum_fusion), calls=%async_computation | async-start | bytes 27262976 | tf_op jit(solution)/shard_map/all_to_all | solution.py:47
  172.6 0.0 all-gather.3.cloned.1.call-start
  172.7 9.5 %mul.107 = f32[512,104,128]{2,1,0:T(8,128)} broadcast(f32[512,104]{1,0:T(8,128)S(1)} %bitcast.54), dimensions={0,1} | broadcast | bytes 27475968 | tf_op jit(solution)/shard_map/mul | solution.py:30
  182.2 27.5 %mul.108 = f32[8,64,13312]{2,1,0:T(8,128)} reshape(f32[512,104,128]{2,1,0:T(8,128)} %mul.107) | data formatting | bytes 54525952 | tf_op jit(solution)/shard_map/mul | solution.py:30
  209.7 113.1 %all-to-all-done = bf16[8,64,13312]{2,1,0:T(8,128)(2,1)} async-done(((bf16[8,64,13312]{2,1,0:T(8,128)(2,1)}), bf16[8,64,13312]{2,1,0:T(8,128)(2,1)}, u32[]{:S(2)}, u32[]{:S(2)}) %all-to-all-start) | async-done | bytes 13631520 | tf_op jit(solution)/shard_map/all_to_all | solution.py:47
  322.8 14.5 %multiply_reduce_fusion = f32[64,13312]{1,0:T(8,128)S(1)} fusion(f32[8,64,13312]{2,1,0:T(8,128)} %mul.108, bf16[8,64,13312]{2,1,0:T(8,128)(2,1)} %all-to-all-done), kind=kLoop, calls=%fused_computation.6 | loop fusion | flops 19595264 | bytes 44302336 | tf_op jit(solution)/shard_map/reduce_sum | solution.py:50
  337.4 1.6 fusion.9
  339.0 2.6 abs.23
  341.6 2.0 reduce_max.29
  343.7 0.5 mul.112
  344.2 1.5 fusion.7
  345.7 0.0 all-gather.3.cloned.1.call-update
  345.7 0.0 all-reduce.2.cloned.1.call-start
  345.8 19.6 %fusion = bf16[6656,2048]{1,0:T(8,128)(2,1)} fusion(bf16[6656,2048]{1,0:T(8,128)(2,1)} %param.12, f32[52,2048]{1,0:T(8,128)} %param.13), kind=kLoop, calls=%fused_computation.1 | loop fusion | flops 40894464 | bytes 54951936 | tf_op jit(solution)/shard_map/convert_element_type | solution.py:14
  365.4 0.1 copy.38
  365.5 8.5 %all-gather = bf16[8,64,52]{1,2,0:T(8,128)(2,1)S(1)} all-gather(bf16[1,64,52]{1,2,0:T(8,128)(2,1)S(1)} %copy.38), channel_id=1, replica_groups=mesh['mp'=8,'hidden'=4] {'mp'}, dimensions={0}, use_global_device_ids=true | all-gather | bytes 59904 | tf_op jit(solution)/shard_map/all_gather | solution.py:55
  374.0 0.1 reshape.78
  374.1 6.6 %mul.115 = f32[512,52,128]{0,2,1:T(8,128)} broadcast(f32[512,52]{0,1:T(8,128)S(1)} %reshape.78), dimensions={0,1} | broadcast | bytes 13737984 | tf_op jit(solution)/shard_map/mul | solution.py:30
  380.7 14.6 %copy.40 = f32[512,6656]{1,0:T(8,128)} copy(f32[512,6656]{0,1:T(8,128)} %bitcast.48) | data formatting | bytes 27262976 | tf_op jit(solution)/shard_map/mul | solution.py:30
  395.3 0.0 copy-start.1
  395.3 0.0 all-gather.3.cloned.1.call-done
  395.3 26.2 %fusion.6 = bf16[512,2048]{1,0:T(8,128)(2,1)} fusion(bf16[6656,2048]{1,0:T(8,128)(2,1)} %fusion, f32[512,6656]{1,0:T(8,128)} %copy.40, bf16[512,6656]{1,0:T(8,128)(2,1)} %all-gather.3.cloned.1.call-done), kind=kOutput, calls=%fused_computation.17 | convolution fusion | flops 13969915904 | bytes 49807360 | tf_op jit(solution)/shard_map/dot_general | solution.py:60
  421.5 0.0 all-reduce.2.cloned.1.call-update
  421.5 86.4 %all-reduce.2.cloned.1.call-done = bf16[512,2048]{1,0:T(8,128)(2,1)} async-done(((bf16[512,2048]{1,0:T(8,128)(2,1)}), bf16[512,2048]{1,0:T(8,128)(2,1)}) %all-reduce.2.cloned.1.call-update) | async-done | bytes 2097168 | tf_op jit(solution)/shard_map/psum | solution.py:59
  508.0 0.0 copy-done.1
  508.0 3.7 add_convert_fusion
  (5 shorter events, 0.1 us)
Async XLA Ops:
  6.5 19.5 %copy-start = (bf16[512,2048]{1,0:T(8,128)(2,1)S(1)}, bf16[512,2048]{1,0:T(8,128)(2,1)}, u32[]{:S(2)}) copy-start(bf16[512,2048]{1,0:T(8,128)(2,1)} %param.7) | copy-start | bytes 6291460
  51.3 7.3 %copy-start.2 = (f32[16,6656]{1,0:T(8,128)S(1)}, f32[16,6656]{1,0:T(8,128)}, u32[]{:S(2)}) copy-start(f32[16,6656]{1,0:T(8,128)} %param.11) | copy-start | bytes 1277956
  111.0 56.1 %all-to-all-start.1 = ((bf16[8,64,104]{2,1,0:T(8,128)(2,1)}), bf16[8,64,104]{2,1,0:T(8,128)(2,1)S(1)}, u32[]{:S(2)}, u32[]{:S(2)}) async-start(bf16[8,64,104]{2,1,0:T(8,128)(2,1)} %pad_maximum_fusion.1), calls=%async_computation.1 | async-start | bytes 262144 | tf_op jit(solution)/shard_map/all_to_all | solution.py:48
  167.1 155.7 %all-to-all-start = ((bf16[8,64,13312]{2,1,0:T(8,128)(2,1)}), bf16[8,64,13312]{2,1,0:T(8,128)(2,1)}, u32[]{:S(2)}, u32[]{:S(2)}) async-start(bf16[8,64,13312]{2,1,0:T(8,128)(2,1)} %pad_maximum_fusion), calls=%async_computation | async-start | bytes 27262976 | tf_op jit(solution)/shard_map/all_to_all | solution.py:47
  172.6 222.7 %all-gather.3.cloned.1.call-start = ((), (), s32[]{:S(2)}) async-start(), calls=%async_computation.2 | async-start | bytes 7667712 | tf_op jit(solution)/shard_map/all_gather | solution.py:54
  345.7 162.2 %all-reduce.2.cloned.1.call-start = ((), (), s32[]{:S(2)}) async-start(), calls=%async_computation.3 | async-start | bytes 4194304 | tf_op jit(solution)/shard_map/psum | solution.py:59
  395.3 112.7 %copy-start.1 = (bf16[512,2048]{1,0:T(8,128)(2,1)S(1)}, bf16[512,2048]{1,0:T(8,128)(2,1)}, u32[]{:S(2)}) copy-start(bf16[512,2048]{1,0:T(8,128)(2,1)} %param.7) | copy-start | bytes 6291460
Sparse Core Ops, SparseCore 0:
  345.9 47.1 all-gather.2
  421.7 86.2 all-reduce.1
where the time goes:
time: 521 us; the launch traced here: 519 us
  waiting for transfers between devices  200 us (38%)
  other arithmetic  128 us (25%)
  local copies, waits for them, and re-layouts  81.6 us (16%)
  matrix products  76.9 us (15%)
  between operations  13.5 us (3%)
  starting transfers between devices  10.8 us (2%)
  blocking collectives  8.49 us (2%)
    all_to_all x1, waiting for transfers between devices, body(): lax.all_to_all(codes, 'mp', split_axis=0, concat_axis=0, tiled=True)  113 us
    psum x1, waiting for transfers between devices, body(): lax.psum(jnp.dot(activation, down_w, preferred_element_type=jnp.float32)....  86.4 us
    mul x4, local copies, waits for them, and re-layouts, decode(): return (blocks * step_size[..., None]).reshape(row_count, columns)  58.2 us
    convert_element_type x3, other arithmetic, dequantize(): (blocks * scales[:, None, :]).reshape(depth, columns).astype(jnp.bfloat16)  58.1 us
    dot_general x1, matrix products, body(): jnp.dot(activation, down_w, preferred_element_type=jnp.float32)  26.2 us
    dot_general x1, matrix products, body(): up_part = jnp.dot(states, up_w, preferred_element_type=jnp.float32)  25.5 us
    dot_general x1, matrix products, body(): gate_part = jnp.dot(states, gate_w, preferred_element_type=jnp.float32)  25.2 us
    convert_element_type x3, other arithmetic, encode(): codes = (blocks * factor[..., None]).astype(jnp.bfloat16)  20.8 us
  transfers between devices with their start and end apart: 4, of which 2 were waited for; matrix products, arithmetic and copies ran while one was open for 25% of the time, Pallas kernels for 0%

commit v1 on v0

--- a/solution.py
+++ b/solution.py
@@ -5,6 +5,11 @@
 
 BLOCK = 128
 epsilon = 1e-06
+
+
+def gather_and_add(block, axis):
+    shards = lax.all_gather(block, axis)
+    return jnp.sum(shards, axis=0)
 
 
 def dequantize(quantized, scales):
@@ -56,7 +61,7 @@
     )
     activation = decode(all_codes, all_scales).astype(jnp.bfloat16)
     down_w = dequantize(down_codes, down_scales)
-    whole_sum = lax.psum(
+    whole_sum = gather_and_add(
         jnp.dot(activation, down_w, preferred_element_type=jnp.float32).astype(jnp.bfloat16),
         "hidden",
     ).astype(jnp.float32)

time: 521 us -> 597 us (1.15)
  waiting for transfers between devices: 200 us -> 263 us
    all_gather x0 -> x1, waiting for transfers between devices: none -> 150 us  [gather_and_add(): shards = lax.all_gather(block, axis)]
    psum x1 -> x0, waiting for transfers between devices: 86.4 us -> none  [body(): lax.psum(jnp.dot(activation, down_w, preferred_element_type=jnp.float32)....]
  transfers between devices with their start and end apart: 4 -> 4, of which waited for: 2 -> 2; matrix products, arithmetic and copies ran while one was open for 25% -> 22% of each run, Pallas kernels for 0% -> 0%
where the time goes in v1:
time: 597 us; the launch traced here: 589 us
  waiting for transfers between devices  263 us (44%)
  other arithmetic  133 us (22%)
  local copies, waits for them, and re-layouts  81.9 us (14%)
  matrix products  77.2 us (13%)
  between operations  13.7 us (2%)
  starting transfers between devices  11 us (2%)
  blocking collectives  8.5 us (1%)
    all_gather x1, waiting for transfers between devices, gather_and_add(): shards = lax.all_gather(block, axis)  150 us
    all_to_all x1, waiting for transfers between devices, body(): lax.all_to_all(codes, 'mp', split_axis=0, concat_axis=0, tiled=True)  113 us
    mul x4, local copies, waits for them, and re-layouts, decode(): return (blocks * step_size[..., None]).reshape(row_count, columns)  58.3 us
    convert_element_type x3, other arithmetic, dequantize(): (blocks * scales[:, None, :]).reshape(depth, columns).astype(jnp.bfloat16)  58.2 us
    dot_general x1, matrix products, body(): jnp.dot(activation, down_w, preferred_element_type=jnp.float32)  26.3 us
    dot_general x1, matrix products, body(): up_part = jnp.dot(states, up_w, preferred_element_type=jnp.float32)  25.7 us
    dot_general x1, matrix products, body(): gate_part = jnp.dot(states, gate_w, preferred_element_type=jnp.float32)  25.2 us
    convert_element_type x3, other arithmetic, encode(): codes = (blocks * factor[..., None]).astype(jnp.bfloat16)  20.8 us
  transfers between devices with their start and end apart: 4, of which 2 were waited for; matrix products, arithmetic and copies ran while one was open for 22% of the time, Pallas kernels for 0%

profile of v1, /device:TPU:0, one launch (start us, length us, event | category | flops | bytes accessed | tf_op | source)
XLA Modules:
  0.0 588.8 jit_solution(9852118269134284058)
XLA Ops:
  6.5 0.0 copy-start
  6.5 19.5 %fusion.2 = bf16[2048,6656]{1,0:T(8,128)(2,1)} fusion(bf16[2048,6656]{1,0:T(8,128)(2,1)} %param.8, f32[16,6656]{1,0:T(8,128)} %param.9), kind=kLoop, calls=%fused_computation.5 | loop fusion | flops 40894464 | bytes 54951936 | tf_op jit(solution)/shard_map/convert_element_type | solution.py:19
  26.1 0.0 copy-done
  26.1 25.2 %bitcast_abs_fusion.1 = (f32[512,6656]{0,1:T(8,128)}, f32[6656,512]{1,0:T(8,128)}) fusion(bf16[2048,6656]{1,0:T(8,128)(2,1)} %fusion.2, bf16[512,2048]{1,0:T(8,128)(2,1)S(1)} %copy-done), kind=kOutput, calls=%fused_computation.13 | convolution fusion | flops 13962051584 | bytes 56623104 | tf_op jit(solution)/shard_map/dot_general | solution.py:45
  51.3 0.0 copy-start.1
  51.3 7.1 %reduce_max.27 = f32[512,52]{0,1:T(8,128)S(1)} reduce(f32[512,52,128]{0,2,1:T(8,128)} %bitcast.52, f32[]{:T(128)} %constant.4.clone.1), dimensions={2}, to_apply=%region_0.0 | reduce | flops 3381248 | bytes 13737988 | tf_op jit(solution)/shard_map/reduce_max | solution.py:25
  58.4 0.1 copy.41
  58.5 0.0 copy-done.1
  58.5 19.1 %fusion.1 = bf16[2048,6656]{1,0:T(8,128)(2,1)} fusion(bf16[2048,6656]{1,0:T(8,128)(2,1)} %param.10, f32[16,6656]{1,0:T(8,128)S(1)} %copy-done.1), kind=kLoop, calls=%fused_computation.3 | loop fusion | flops 40894464 | bytes 54951936 | tf_op jit(solution)/shard_map/convert_element_type | solution.py:19
  77.6 25.7 %bitcast_abs_fusion = (f32[512,6656]{0,1:T(8,128)}, f32[6656,512]{1,0:T(8,128)}) fusion(bf16[2048,6656]{1,0:T(8,128)(2,1)} %fusion.1, bf16[512,2048]{1,0:T(8,128)(2,1)S(1)} %copy-done), kind=kOutput, calls=%fused_computation.10 | convolution fusion | flops 13962051584 | bytes 56623104 | tf_op jit(solution)/shard_map/dot_general | solution.py:46
  103.4 7.0 %reduce_max.28 = f32[512,52]{0,1:T(8,128)S(1)} reduce(f32[512,52,128]{0,2,1:T(8,128)} %bitcast.53, f32[]{:T(128)} %constant.4.clone.1), dimensions={2}, to_apply=%region_1.0 | reduce | flops 3381248 | bytes 13737988 | tf_op jit(solution)/shard_map/reduce_max | solution.py:25
  110.4 0.1 copy.42
  110.6 0.8 pad_maximum_fusion.1
  111.3 5.4 all-to-all-start.1
  116.8 9.7 %fusion.4 = bf16[512,6656]{0,1:T(8,128)(2,1)} fusion(f32[6656,512]{1,0:T(8,128)} %get-tuple-element.14, f32[512,52]{0,1:T(8,128)S(1)} %get-tuple-element.5), kind=kLoop, calls=%fused_computation.12 | loop fusion | flops 6815744 | bytes 20553728 | tf_op jit(solution)/shard_map/convert_element_type | solution.py:27
  126.5 10.0 %copy.34 = bf16[512,6656]{1,0:T(8,128)(2,1)} copy(bf16[512,6656]{0,1:T(8,128)(2,1)} %fusion.4) | data formatting | bytes 13631488 | tf_op jit(solution)/shard_map/convert_element_type | solution.py:27
  136.4 9.6 %fusion.3 = bf16[512,6656]{0,1:T(8,128)(2,1)} fusion(f32[6656,512]{1,0:T(8,128)} %get-tuple-element.12, f32[512,52]{0,1:T(8,128)S(1)} %get-tuple-element.7), kind=kLoop, calls=%fused_computation.9 | loop fusion | flops 6815744 | bytes 20553728 | tf_op jit(solution)/shard_map/convert_element_type | solution.py:27
  146.0 10.0 %copy.35 = bf16[512,6656]{1,0:T(8,128)(2,1)} copy(bf16[512,6656]{0,1:T(8,128)(2,1)} %fusion.3) | data formatting | bytes 13631488 | tf_op jit(solution)/shard_map/convert_element_type | solution.py:27
  156.0 11.8 %pad_maximum_fusion = bf16[8,64,13312]{2,1,0:T(8,128)(2,1)} fusion(bf16[8,64,6656]{2,1,0:T(8,128)(2,1)} %bitcast.51, bf16[8,64,6656]{2,1,0:T(8,128)(2,1)} %bitcast.50), kind=kLoop, calls=%fused_computation.7 | loop fusion | flops 27262976 | bytes 27262976 | tf_op jit(solution)/shard_map/concatenate | solution.py:49
  167.8 0.0 all-to-all-done.1
  167.8 5.5 all-to-all-start
  173.3 0.0 all-gather.5.cloned.1.call-start
  173.4 9.5 %mul.107 = f32[512,104,128]{2,1,0:T(8,128)} broadcast(f32[512,104]{1,0:T(8,128)S(1)} %bitcast.56), dimensions={0,1} | broadcast | bytes 27475968 | tf_op jit(solution)/shard_map/mul | solution.py:35
  182.9 27.5 %mul.108 = f32[8,64,13312]{2,1,0:T(8,128)} reshape(f32[512,104,128]{2,1,0:T(8,128)} %mul.107) | data formatting | bytes 54525952 | tf_op jit(solution)/shard_map/mul | solution.py:35
  210.4 113.1 %all-to-all-done = bf16[8,64,13312]{2,1,0:T(8,128)(2,1)} async-done(((bf16[8,64,13312]{2,1,0:T(8,128)(2,1)}), bf16[8,64,13312]{2,1,0:T(8,128)(2,1)}, u32[]{:S(2)}, u32[]{:S(2)}) %all-to-all-start) | async-done | bytes 13631520 | tf_op jit(solution)/shard_map/all_to_all | solution.py:52
  323.5 14.5 %multiply_reduce_fusion = f32[64,13312]{1,0:T(8,128)S(1)} fusion(f32[8,64,13312]{2,1,0:T(8,128)} %mul.108, bf16[8,64,13312]{2,1,0:T(8,128)(2,1)} %all-to-all-done), kind=kLoop, calls=%fused_computation.6 | loop fusion | flops 19595264 | bytes 44302336 | tf_op jit(solution)/shard_map/reduce_sum | solution.py:55
  338.1 1.6 fusion.9
  339.7 2.6 abs.23
  342.3 2.0 reduce_max.29
  344.4 0.5 mul.112
  344.9 1.5 fusion.7
  346.4 0.0 all-gather.5.cloned.1.call-update
  346.4 0.0 all-gather.7.cloned.1.call-start
  346.5 19.6 %fusion = bf16[6656,2048]{1,0:T(8,128)(2,1)} fusion(bf16[6656,2048]{1,0:T(8,128)(2,1)} %param.12, f32[52,2048]{1,0:T(8,128)} %param.13), kind=kLoop, calls=%fused_computation.1 | loop fusion | flops 40894464 | bytes 54951936 | tf_op jit(solution)/shard_map/convert_element_type | solution.py:19
  366.1 0.1 copy.38
  366.2 8.5 %all-gather.1 = bf16[8,64,52]{1,2,0:T(8,128)(2,1)S(1)} all-gather(bf16[1,64,52]{1,2,0:T(8,128)(2,1)S(1)} %copy.38), channel_id=1, replica_groups=mesh['mp'=8,'hidden'=4] {'mp'}, dimensions={0}, use_global_device_ids=true | all-gather | bytes 59904 | tf_op jit(solution)/shard_map/all_gather | solution.py:60
  374.7 0.1 reshape.79
  374.8 6.6 %mul.115 = f32[512,52,128]{0,2,1:T(8,128)} broadcast(f32[512,52]{0,1:T(8,128)S(1)} %reshape.79), dimensions={0,1} | broadcast | bytes 13737984 | tf_op jit(solution)/shard_map/mul | solution.py:35
  381.4 14.7 %copy.40 = f32[512,6656]{1,0:T(8,128)} copy(f32[512,6656]{0,1:T(8,128)} %bitcast.49) | data formatting | bytes 27262976 | tf_op jit(solution)/shard_map/mul | solution.py:35
  396.1 0.0 all-gather.5.cloned.1.call-done
  396.1 26.3 %fusion.6 = bf16[512,2048]{1,0:T(8,128)(2,1)} fusion(bf16[6656,2048]{1,0:T(8,128)(2,1)} %fusion, f32[512,6656]{1,0:T(8,128)} %copy.40, bf16[512,6656]{1,0:T(8,128)(2,1)} %all-gather.5.cloned.1.call-done), kind=kOutput, calls=%fused_computation.17 | convolution fusion | flops 13969915904 | bytes 49807360 | tf_op jit(solution)/shard_map/dot_general | solution.py:65
  422.3 0.0 all-gather.7.cloned.1.call-update
  422.3 150.0 %all-gather.7.cloned.1.call-done = bf16[2048,2048]{1,0:T(8,128)(2,1)} async-done(((bf16[512,2048]{1,0:T(8,128)(2,1)}), bf16[2048,2048]{1,0:T(8,128)(2,1)}) %all-gather.7.cloned.1.call-update) | async-done | bytes 8388624 | tf_op jit(solution)/shard_map/all_gather | solution.py:11
  572.3 5.7 reduce_sum.22
  578.0 3.7 add_convert_fusion
  (5 shorter events, 0.1 us)
Async XLA Ops:
  6.5 19.5 %copy-start = (bf16[512,2048]{1,0:T(8,128)(2,1)S(1)}, bf16[512,2048]{1,0:T(8,128)(2,1)}, u32[]{:S(2)}) copy-start(bf16[512,2048]{1,0:T(8,128)(2,1)} %param.7) | copy-start | bytes 6291460
  51.3 7.3 %copy-start.1 = (f32[16,6656]{1,0:T(8,128)S(1)}, f32[16,6656]{1,0:T(8,128)}, u32[]{:S(2)}) copy-start(f32[16,6656]{1,0:T(8,128)} %param.11) | copy-start | bytes 1277956
  111.3 56.5 %all-to-all-start.1 = ((bf16[8,64,104]{2,1,0:T(8,128)(2,1)}), bf16[8,64,104]{2,1,0:T(8,128)(2,1)S(1)}, u32[]{:S(2)}, u32[]{:S(2)}) async-start(bf16[8,64,104]{2,1,0:T(8,128)(2,1)} %pad_maximum_fusion.1), calls=%async_computation.1 | async-start | bytes 262144 | tf_op jit(solution)/shard_map/all_to_all | solution.py:53
  167.8 155.7 %all-to-all-start = ((bf16[8,64,13312]{2,1,0:T(8,128)(2,1)}), bf16[8,64,13312]{2,1,0:T(8,128)(2,1)}, u32[]{:S(2)}, u32[]{:S(2)}) async-start(bf16[8,64,13312]{2,1,0:T(8,128)(2,1)} %pad_maximum_fusion), calls=%async_computation | async-start | bytes 27262976 | tf_op jit(solution)/shard_map/all_to_all | solution.py:52
  173.3 222.8 %all-gather.5.cloned.1.call-start = ((), (), s32[]{:S(2)}) async-start(), calls=%async_computation.2 | async-start | bytes 7667712 | tf_op jit(solution)/shard_map/all_gather | solution.py:59
  346.4 225.9 %all-gather.7.cloned.1.call-start = ((), (), s32[]{:S(2)}) async-start(), calls=%async_computation.3 | async-start | bytes 10485760 | tf_op jit(solution)/shard_map/all_gather | solution.py:11
Sparse Core Ops, SparseCore 0:
  346.5 47.1 all-gather.4
  422.5 149.7 all-gather.6
